TPU v7x, 32 devices: a whole 2x2x4 slice. The times are simulated.
32 devices in a mesh: aa: 8 (over z, y), ba: 4 (over x, core).
Axes of the slice: x: 2, y: 2, z: 4, core: 2. Of those that a mesh axis runs over, the one named last changes fastest.
Arguments:
- tokens: bfloat16 [4096, 8192], P('aa', 'ba'), may hold values from -6 to 6
- request_adapter_index: int32 [4096, 1], P('aa'), may hold values from 0 to 127; in each aligned block of 512 rows (0 to 511, 512 to 1023, ...) at most 8 rows name the same one
- key_weight: bfloat16 [8192, 1024], P('ba'), may hold values from -0.0625 to 0.0625
- value_weight: bfloat16 [8192, 1024], P('ba'), may hold values from -0.0625 to 0.0625
- adapter_down_weight: bfloat16 [128, 32, 8192], P('aa', None, 'ba'), may hold values from -0.0625 to 0.0625
- adapter_up_weight: bfloat16 [128, 2, 16, 1024], P('aa'), may hold values from -1.5 to 1.5
Outputs:
- keys_out: bfloat16 [4096, 1024], P('aa', 'ba')
- values_out: bfloat16 [4096, 1024], P('aa', 'ba')
Inputs may be any that keep to these rules, and one draw needn't show every extreme that they name: `request_adapter_index`: among the 512 rows of one device no adapter is named more than 8 times, a bound that some block reaches.
All inputs are finite; a program needn't handle non-finite values.
Results may differ from a plain program's by a relative error of at most 0.001.
Values may be sent and summed in bfloat16 or wider, within the bound.
A program may use at most 128 MiB of HBM per device.

v0:
```python
import jax
import jax.numpy as jnp
from jax import lax
from jax.sharding import PartitionSpec as P


def on_device(
    tokens, request_adapter_index, key_weight, value_weight, adapter_down_weight, adapter_up_weight
):
    bank_count = lax.axis_size("aa")
    split_count = lax.axis_size("ba")
    tok_rows, width_local = tokens.shape
    resident_adapters, twice_rank, spare_width = adapter_down_weight.shape
    rank_width = twice_rank // 2
    kv_width = key_weight.shape[1]
    kv_local = kv_width // split_count
    adapters_all = resident_adapters * bank_count
    capacity = max(2, 2 * tok_rows // adapters_all)
    slot_total = adapters_all * capacity
    selected_adapter = request_adapter_index[:, 0]
    positions = jnp.arange(tok_rows, dtype=jnp.int32)
    same_adapter = (selected_adapter[:, None] == selected_adapter[None, :]) & (
        positions[None, :] < positions[:, None]
    )
    earlier = jnp.sum(same_adapter.astype(jnp.int32), axis=1)
    slot_of = selected_adapter * capacity + earlier
    source = jnp.zeros((slot_total,), jnp.int32).at[slot_of].set(positions)
    outgoing = tokens[source].reshape(bank_count, resident_adapters, capacity, width_local)
    complete_up_weight = adapter_up_weight.astype(jnp.float32)
    offset = lax.axis_index("ba") * kv_local
    up_used = lax.dynamic_slice_in_dim(complete_up_weight, offset, kv_local, 3)
    partial_rank = jnp.einsum(
        "sakd,ajd->sakj",
        lax.all_to_all(outgoing, "aa", split_axis=0, concat_axis=0, tiled=True),
        adapter_down_weight,
        preferred_element_type=jnp.float32,
    )
    rank_sum = lax.psum(partial_rank, "ba")
    key_change = jnp.einsum(
        "sakr,arc->sakc", rank_sum[..., :rank_width], up_used[:, 0], precision=lax.Precision.HIGHEST
    )
    value_change = jnp.einsum(
        "sakr,arc->sakc", rank_sum[..., rank_width:], up_used[:, 1], precision=lax.Precision.HIGHEST
    )
    key_change, value_change = (key_change, value_change)
    changes = jnp.concatenate([key_change, value_change], axis=3)
    returned = lax.all_to_all(changes, "aa", split_axis=0, concat_axis=0, tiled=True)
    per_token = returned.reshape(slot_total, returned.shape[3])[slot_of]
    key_part = jnp.dot(tokens, key_weight, preferred_element_type=jnp.float32)
    value_part = jnp.dot(tokens, value_weight, preferred_element_type=jnp.float32)
    base_part = jnp.stack(
        [
            key_part.reshape(tok_rows, split_count, kv_local),
            value_part.reshape(tok_rows, split_count, kv_local),
        ],
        axis=2,
    )
    base_part = base_part.reshape(tok_rows, 2 * kv_width)
    summed = lax.psum_scatter(base_part, "ba", scatter_dimension=1, tiled=True) + per_token
    return (summed[:, :kv_local].astype(jnp.bfloat16), summed[:, kv_local:].astype(jnp.bfloat16))


def solution(mesh):
    return jax.shard_map(
        on_device,
        mesh=mesh,
        in_specs=(
            P("aa", "ba"),
            P("aa", None),
            P("ba", None),
            P("ba", None),
            P("aa", None, "ba"),
            P("aa", None, None, None),
        ),
        out_specs=(P("aa", "ba"), P("aa", "ba")),
        check_vma=False,
    )
```

profile of v0, /device:TPU:0, one launch (start us, length us, event | category | flops | bytes accessed | tf_op | source)
XLA Modules:
  0.0 226.5 jit_solution(3691659439120171811)
XLA Ops:
  7.2 0.0 copy-start
  7.2 1.1 convert_reduce_fusion
  8.3 0.7 compare_select_fusion
  9.0 2.4 %scatter_custom_fusion = s32[1024]{0:T(1024)S(1)} fusion(s32[512]{0:T(512)S(1)} %bitcast.40, s32[512]{0:T(512)S(1)} %iota.9, s32[]{:T(128)} %constant.6.clone.1), kind=kCustom, calls=%fused_computation.23 | custom fusion | bytes 4100 | tf_op jit(solution)/shard_map/scatter | solution.py:27
  11.4 0.0 copy-done
  11.4 6.0 %gather_fusion = bf16[1024,2048]{1,0:T(8,128)(2,1)} fusion(bf16[512,2048]{1,0:T(8,128)(2,1)S(1)} %copy-done, s32[1024]{0:T(1024)S(1)} %fusion.11), kind=kCustom, calls=%fused_computation | custom fusion | bytes 8392704 | tf_op jit(solution)/shard_map/gather | solution.py:28
  17.5 7.3 %all-to-all-start = ((bf16[8,16,8,2048]{3,2,1,0:T(8,128)(2,1)}), bf16[8,16,8,2048]{3,2,1,0:T(8,128)(2,1)}, u32[]{:S(2)}, u32[]{:S(2)}) async-start(bf16[8,16,8,2048]{3,2,1,0:T(8,128)(2,1)} %bitcast.38), calls=%async_computation.1 | async-start | bytes 8388608 | tf_op jit(solution)/shard_map/all_to_all | solution.py:34
  24.8 0.0 all-reduce.2.cloned.1.call-start
  24.8 5.8 %fusion.17 = f32[512,1024]{1,0:T(8,128)} fusion(bf16[512,2048]{1,0:T(8,128)(2,1)S(1)} %copy-done, bf16[2048,1024]{1,0:T(8,128)(2,1)} %param.8), kind=kOutput, calls=%fused_computation.28 | convolution fusion | flops 2147483648 | bytes 8388608 | tf_op jit(solution)/shard_map/dot_general | solution.py:49
  30.6 3.1 %stack_reshape.6 = f32[512,4,1,256]{3,1,0,2:T(4,128)} reshape(f32[512,1024]{1,0:T(8,128)} %fusion.17) | data formatting | bytes 4194304 | tf_op jit(solution)/shard_map/stack;reshape | solution.py:51
  33.8 5.9 %fusion.18 = f32[512,1024]{1,0:T(8,128)} fusion(bf16[512,2048]{1,0:T(8,128)(2,1)S(1)} %copy-done, bf16[2048,1024]{1,0:T(8,128)(2,1)} %param.9), kind=kOutput, calls=%fused_computation.29 | convolution fusion | flops 2147483648 | bytes 8388608 | tf_op jit(solution)/shard_map/dot_general | solution.py:50
  39.6 3.2 %stack_reshape.7 = f32[512,4,1,256]{3,1,0,2:T(4,128)} reshape(f32[512,1024]{1,0:T(8,128)} %fusion.18) | data formatting | bytes 4194304 | tf_op jit(solution)/shard_map/stack;reshape | solution.py:51
  42.8 75.3 %all-to-all-done = bf16[8,16,8,2048]{3,2,1,0:T(8,128)(2,1)} async-done(((bf16[8,16,8,2048]{3,2,1,0:T(8,128)(2,1)}), bf16[8,16,8,2048]{3,2,1,0:T(8,128)(2,1)}, u32[]{:S(2)}, u32[]{:S(2)}) %all-to-all-start) | async-done | bytes 4194336 | tf_op jit(solution)/shard_map/all_to_all | solution.py:34
  118.1 4.9 %fusion.3 = f32[8,16,8,32]{3,2,0,1:T(8,128)} fusion(bf16[16,32,2048]{2,1,0:T(8,128)(2,1)} %param.10, bf16[8,16,8,2048]{3,2,1,0:T(8,128)(2,1)} %all-to-all-done), kind=kOutput, calls=%fused_computation.10 | convolution fusion | flops 134217728 | bytes 6422528 | tf_op jit(solution)/shard_map/sakd,ajd->sakj/dot_general | solution.py:32
  123.0 0.0 all-reduce.2.cloned.1.call-update
  123.0 0.2 reduce-scatter.2.cloned.1.call-start
  123.2 3.2 %pad_maximum_fusion = f32[512,4,2,256]{3,1,0,2:T(4,128)S(1)} fusion(f32[512,4,1,256]{3,1,0,2:T(4,128)} %stack_reshape.7, f32[512,4,1,256]{3,1,0,2:T(4,128)} %stack_reshape.6), kind=kLoop, calls=%fused_computation.3 | loop fusion | flops 1048576 | bytes 8388608 | tf_op jit(solution)/shard_map/stack | solution.py:51
  126.4 5.2 %copy.18 = f32[512,4,2,256]{3,2,1,0:T(2,128)} copy(f32[512,4,2,256]{3,1,0,2:T(4,128)S(1)} %pad_maximum_fusion) | data formatting | bytes 8388608 | tf_op jit(solution)/shard_map/stack | solution.py:51
  131.6 6.4 %reshape.15 = f32[512,2048]{1,0:T(8,128)} reshape(f32[512,4,2,256]{3,2,1,0:T(2,128)} %copy.18) | data formatting | bytes 8388608 | tf_op jit(solution)/shard_map/reshape | solution.py:58
  138.1 0.0 reduce-scatter.2.cloned.1.call-update
  138.1 17.5 %all-reduce.2.cloned.1.call-done = f32[8,16,8,32]{3,2,0,1:T(8,128)} async-done(((f32[8,16,8,32]{3,2,0,1:T(8,128)}), f32[8,16,8,32]{3,2,0,1:T(8,128)}) %all-reduce.2.cloned.1.call-update) | async-done | bytes 131088 | tf_op jit(solution)/shard_map/psum | solution.py:38
  155.6 1.7 convolution_bitcast_fusion.1
  157.3 1.8 convolution_bitcast_fusion
  159.1 0.3 pad_maximum_fusion.1
  159.4 1.5 copy.21
  160.9 5.5 %all-to-all-start.1 = ((f32[8,16,8,512]{3,2,1,0:T(8,128)}), f32[8,16,8,512]{3,2,1,0:T(8,128)}, u32[]{:S(2)}, u32[]{:S(2)}) async-start(f32[8,16,8,512]{3,2,1,0:T(8,128)} %copy.21), calls=%async_computation.2 | async-start | bytes 4194304 | tf_op jit(solution)/shard_map/all_to_all | solution.py:47
  166.4 47.4 %all-to-all-done.1 = f32[8,16,8,512]{3,2,1,0:T(8,128)} async-done(((f32[8,16,8,512]{3,2,1,0:T(8,128)}), f32[8,16,8,512]{3,2,1,0:T(8,128)}, u32[]{:S(2)}, u32[]{:S(2)}) %all-to-all-start.1) | async-done | bytes 2097184 | tf_op jit(solution)/shard_map/all_to_all | solution.py:47
  213.8 3.6 %gather_fusion.1 = f32[512,512]{1,0:T(8,128)S(1)} fusion(f32[1024,512]{1,0:T(8,128)} %bitcast.15, s32[1024]{0:T(1024)S(1)} %pad_clamp_fusion), kind=kCustom, calls=%fused_computation.1 | custom fusion | bytes 2099200 | tf_op jit(solution)/shard_map/gather | solution.py:48
  217.4 0.0 reduce-scatter.2.cloned.1.call-done
  217.4 1.4 add_convert_fusion
  218.8 0.8 fusion.16
  (3 shorter events, 0.0 us)
Async XLA Ops:
  7.2 4.3 %copy-start = (bf16[512,2048]{1,0:T(8,128)(2,1)S(1)}, bf16[512,2048]{1,0:T(8,128)(2,1)}, u32[]{:S(2)}) copy-start(bf16[512,2048]{1,0:T(8,128)(2,1)} %param.6) | copy-start | bytes 6291460
  17.5 100.6 %all-to-all-start = ((bf16[8,16,8,2048]{3,2,1,0:T(8,128)(2,1)}), bf16[8,16,8,2048]{3,2,1,0:T(8,128)(2,1)}, u32[]{:S(2)}, u32[]{:S(2)}) async-start(bf16[8,16,8,2048]{3,2,1,0:T(8,128)(2,1)} %bitcast.38), calls=%async_computation.1 | async-start | bytes 8388608 | tf_op jit(solution)/shard_map/all_to_all | solution.py:34
  24.8 130.9 %all-reduce.2.cloned.1.call-start = ((), (), s32[]{:S(2)}) async-start(), calls=%async_computation.4 | async-start | bytes 1048576 | tf_op jit(solution)/shard_map/psum | solution.py:38
  123.0 94.4 %reduce-scatter.2.cloned.1.call-start = ((), (), s32[]{:S(2)}) async-start(), calls=%async_computation.3 | async-start | bytes 5242880 | tf_op jit(solution)/shard_map/reduce_scatter | solution.py:59
  160.9 52.9 %all-to-all-start.1 = ((f32[8,16,8,512]{3,2,1,0:T(8,128)}), f32[8,16,8,512]{3,2,1,0:T(8,128)}, u32[]{:S(2)}, u32[]{:S(2)}) async-start(f32[8,16,8,512]{3,2,1,0:T(8,128)} %copy.21), calls=%async_computation.2 | async-start | bytes 4194304 | tf_op jit(solution)/shard_map/all_to_all | solution.py:47
Sparse Core Ops, SparseCore 0:
  123.1 32.4 all-reduce.1
  158.2 44.5 reduce-scatter.1
where the time goes:
time: 227 us; the launch traced here: 226 us
  waiting for transfers between devices  140 us (62%)
  local copies, waits for them, and re-layouts  32.4 us (14%)
  matrix products  20 us (9%)
  between operations  14.1 us (6%)
  starting transfers between devices  13.1 us (6%)
  other arithmetic  6.65 us (3%)
    all_to_all x1, waiting for transfers between devices, on_device(): lax.all_to_all(outgoing, 'aa', split_axis=0, concat_axis=0, tiled=True)  75.3 us
    all_to_all x1, waiting for transfers between devices, on_device(): lax.all_to_all(changes, 'aa', split_axis=0, concat_axis=0, tiled=True)  47.4 us
    psum x1, waiting for transfers between devices, on_device(): rank_sum = lax.psum(partial_rank, 'ba')  17.5 us
    another operation x3, local copies, waits for them, and re-layouts, on_device(): jnp.stack([key_part.reshape(tok_rows, split_count, kv_local), value_part....  11.5 us
    all_to_all x1, starting transfers between devices, on_device(): lax.all_to_all(outgoing, 'aa', split_axis=0, concat_axis=0, tiled=True)  7.31 us
    reshape x1, local copies, waits for them, and re-layouts, on_device(): base_part = base_part.reshape(tok_rows, 2 * kv_width)  6.43 us
    gather x1, local copies, waits for them, and re-layouts, on_device(): tokens[source].reshape(bank_count, resident_adapters, capacity, width_local)  6.02 us
    dot_general x1, matrix products, on_device(): jnp.dot(tokens, value_weight, preferred_element_type=jnp.float32)  5.85 us
  transfers between devices with their start and end apart: 4, of which 3 were waited for; matrix products, arithmetic and copies ran while one was open for 18% of the time, Pallas kernels for 0%

commit v1 on v0

--- a/solution.py
+++ b/solution.py
@@ -35,7 +35,7 @@
         adapter_down_weight,
         preferred_element_type=jnp.float32,
     )
-    rank_sum = lax.psum(partial_rank, "ba")
+    rank_sum = jnp.sum(lax.all_gather(partial_rank, "ba"), axis=0)
     key_change = jnp.einsum(
         "sakr,arc->sakc", rank_sum[..., :rank_width], up_used[:, 0], precision=lax.Precision.HIGHEST
     )

time: 227 us -> 212 us (0.934)
  waiting for transfers between devices: 140 us -> 109 us
  blocking collectives: 0 us -> 16.3 us
    psum x1 -> x0, waiting for transfers between devices: 17.5 us -> none  [on_device(): rank_sum = lax.psum(partial_rank, 'ba')]
    all_gather x0 -> x1, blocking collectives: none -> 16.3 us  [on_device(): rank_sum = jnp.sum(lax.all_gather(partial_rank, 'ba'), axis=0)]
    all_to_all x1, waiting for transfers between devices: 75.3 us -> 60.4 us  [on_device(): lax.all_to_all(outgoing, 'aa', split_axis=0, concat_axis=0, tiled=True)]
  transfers between devices with their start and end apart: 4 -> 3, of which waited for: 3 -> 2; matrix products, arithmetic and copies ran while one was open for 18% -> 22% of each run, Pallas kernels for 0% -> 0%
where the time goes in v1:
time: 212 us; the launch traced here: 211 us
  waiting for transfers between devices  109 us (51%)
  local copies, waits for them, and re-layouts  32.3 us (15%)
  matrix products  18.8 us (9%)
  blocking collectives  16.3 us (8%)
  between operations  14.1 us (7%)
  starting transfers between devices  11.7 us (6%)
  other arithmetic  8.52 us (4%)
    all_to_all x1, waiting for transfers between devices, on_device(): lax.all_to_all(outgoing, 'aa', split_axis=0, concat_axis=0, tiled=True)  60.4 us
    all_to_all x1, waiting for transfers between devices, on_device(): lax.all_to_all(changes, 'aa', split_axis=0, concat_axis=0, tiled=True)  49 us
    all_gather x1, blocking collectives, on_device(): rank_sum = jnp.sum(lax.all_gather(partial_rank, 'ba'), axis=0)  16.3 us
    another operation x3, local copies, waits for them, and re-layouts, on_device(): jnp.stack([key_part.reshape(tok_rows, split_count, kv_local), value_part....  11.5 us
    all_to_all x1, starting transfers between devices, on_device(): lax.all_to_all(outgoing, 'aa', split_axis=0, concat_axis=0, tiled=True)  7.31 us
    reshape x1, local copies, waits for them, and re-layouts, on_device(): base_part = base_part.reshape(tok_rows, 2 * kv_width)  6.4 us
    gather x1, local copies, waits for them, and re-layouts, on_device(): tokens[source].reshape(bank_count, resident_adapters, capacity, width_local)  6.03 us
    dot_general x1, matrix products, on_device(): jnp.dot(tokens, value_weight, preferred_element_type=jnp.float32)  5.88 us
  transfers between devices with their start and end apart: 3, of which 2 were waited for; matrix products, arithmetic and copies ran while one was open for 22% of the time, Pallas kernels for 0%

profile of v1, /device:TPU:0, one launch (start us, length us, event | category | flops | bytes accessed | tf_op | source)
XLA Modules:
  0.0 211.3 jit_solution(10746339586685548084)
XLA Ops:
  7.2 0.0 copy-start
  7.2 1.1 convert_reduce_fusion
  8.3 0.7 compare_select_fusion
  9.0 2.4 %scatter_custom_fusion = s32[1024]{0:T(1024)S(1)} fusion(s32[512]{0:T(512)S(1)} %bitcast.42, s32[512]{0:T(512)S(1)} %iota.9, s32[]{:T(128)} %constant.7.clone.1), kind=kCustom, calls=%fused_computation.23 | custom fusion | bytes 4100 | tf_op jit(solution)/shard_map/scatter | solution.py:27
  11.4 0.0 copy-done
  11.4 6.0 %gather_fusion = bf16[1024,2048]{1,0:T(8,128)(2,1)} fusion(bf16[512,2048]{1,0:T(8,128)(2,1)S(1)} %copy-done, s32[1024]{0:T(1024)S(1)} %fusion.11), kind=kCustom, calls=%fused_computation | custom fusion | bytes 8392704 | tf_op jit(solution)/shard_map/gather | solution.py:28
  17.5 7.3 %all-to-all-start = ((bf16[8,16,8,2048]{3,2,1,0:T(8,128)(2,1)}), bf16[8,16,8,2048]{3,2,1,0:T(8,128)(2,1)}, u32[]{:S(2)}, u32[]{:S(2)}) async-start(bf16[8,16,8,2048]{3,2,1,0:T(8,128)(2,1)} %bitcast.39), calls=%async_computation.1 | async-start | bytes 8388608 | tf_op jit(solution)/shard_map/all_to_all | solution.py:34
  24.8 0.0 reduce-scatter.2.cloned.1.call-start
  24.8 5.8 %fusion.17 = f32[512,1024]{1,0:T(8,128)} fusion(bf16[512,2048]{1,0:T(8,128)(2,1)S(1)} %copy-done, bf16[2048,1024]{1,0:T(8,128)(2,1)} %param.8), kind=kOutput, calls=%fused_computation.28 | convolution fusion | flops 2147483648 | bytes 8388608 | tf_op jit(solution)/shard_map/dot_general | solution.py:49
  30.6 3.2 %stack_reshape.6 = f32[512,4,1,256]{3,1,0,2:T(4,128)} reshape(f32[512,1024]{1,0:T(8,128)} %fusion.17) | data formatting | bytes 4194304 | tf_op jit(solution)/shard_map/stack;reshape | solution.py:51
  33.8 5.9 %fusion.18 = f32[512,1024]{1,0:T(8,128)} fusion(bf16[512,2048]{1,0:T(8,128)(2,1)S(1)} %copy-done, bf16[2048,1024]{1,0:T(8,128)(2,1)} %param.9), kind=kOutput, calls=%fused_computation.29 | convolution fusion | flops 2147483648 | bytes 8388608 | tf_op jit(solution)/shard_map/dot_general | solution.py:50
  39.7 3.2 %stack_reshape.7 = f32[512,4,1,256]{3,1,0,2:T(4,128)} reshape(f32[512,1024]{1,0:T(8,128)} %fusion.18) | data formatting | bytes 4194304 | tf_op jit(solution)/shard_map/stack;reshape | solution.py:51
  42.8 3.2 %pad_maximum_fusion = f32[512,4,2,256]{3,1,0,2:T(4,128)S(1)} fusion(f32[512,4,1,256]{3,1,0,2:T(4,128)} %stack_reshape.7, f32[512,4,1,256]{3,1,0,2:T(4,128)} %stack_reshape.6), kind=kLoop, calls=%fused_computation.3 | loop fusion | flops 1048576 | bytes 8388608 | tf_op jit(solution)/shard_map/stack | solution.py:51
  46.0 5.2 %copy.18 = f32[512,4,2,256]{3,2,1,0:T(2,128)} copy(f32[512,4,2,256]{3,1,0,2:T(4,128)S(1)} %pad_maximum_fusion) | data formatting | bytes 8388608 | tf_op jit(solution)/shard_map/stack | solution.py:51
  51.2 6.4 %reshape.15 = f32[512,2048]{1,0:T(8,128)} reshape(f32[512,4,2,256]{3,2,1,0:T(2,128)} %copy.18) | data formatting | bytes 8388608 | tf_op jit(solution)/shard_map/reshape | solution.py:58
  57.6 0.0 reduce-scatter.2.cloned.1.call-update
  57.6 60.4 %all-to-all-done = bf16[8,16,8,2048]{3,2,1,0:T(8,128)(2,1)} async-done(((bf16[8,16,8,2048]{3,2,1,0:T(8,128)(2,1)}), bf16[8,16,8,2048]{3,2,1,0:T(8,128)(2,1)}, u32[]{:S(2)}, u32[]{:S(2)}) %all-to-all-start) | async-done | bytes 4194336 | tf_op jit(solution)/shard_map/all_to_all | solution.py:34
  118.1 4.1 %fusion.3 = f32[8,16,8,32]{3,2,0,1:T(8,128)S(1)} fusion(bf16[16,32,2048]{2,1,0:T(8,128)(2,1)} %param.10, bf16[8,16,8,2048]{3,2,1,0:T(8,128)(2,1)} %all-to-all-done), kind=kOutput, calls=%fused_computation.10 | convolution fusion | flops 134217728 | bytes 6422528 | tf_op jit(solution)/shard_map/sakd,ajd->sakj/dot_general | solution.py:32
  122.2 16.3 %all-gather = f32[32,16,8,32]{3,2,0,1:T(8,128)} all-gather(f32[8,16,8,32]{3,2,0,1:T(8,128)S(1)} %fusion.3), channel_id=2, replica_groups=mesh['aa'=8,'ba'=4] {'ba'}, dimensions={0}, use_global_device_ids=true | all-gather | bytes 655360 | tf_op jit(solution)/shard_map/all_gather | solution.py:38
  138.5 1.9 reduce_sum.22
  140.4 1.5 convolution_bitcast_fusion.1
  141.9 1.5 convolution_bitcast_fusion
  143.4 0.3 pad_maximum_fusion.1
  143.7 1.5 copy.21
  145.2 4.3 %all-to-all-start.1 = ((f32[8,16,8,512]{3,2,1,0:T(8,128)}), f32[8,16,8,512]{3,2,1,0:T(8,128)}, u32[]{:S(2)}, u32[]{:S(2)}) async-start(f32[8,16,8,512]{3,2,1,0:T(8,128)} %copy.21), calls=%async_computation.2 | async-start | bytes 4194304 | tf_op jit(solution)/shard_map/all_to_all | solution.py:47
  149.5 49.0 %all-to-all-done.1 = f32[8,16,8,512]{3,2,1,0:T(8,128)} async-done(((f32[8,16,8,512]{3,2,1,0:T(8,128)}), f32[8,16,8,512]{3,2,1,0:T(8,128)}, u32[]{:S(2)}, u32[]{:S(2)}) %all-to-all-start.1) | async-done | bytes 2097184 | tf_op jit(solution)/shard_map/all_to_all | solution.py:47
  198.6 3.6 %gather_fusion.1 = f32[512,512]{1,0:T(8,128)S(1)} fusion(f32[1024,512]{1,0:T(8,128)} %bitcast.16, s32[1024]{0:T(1024)S(1)} %pad_clamp_fusion), kind=kCustom, calls=%fused_computation.1 | custom fusion | bytes 2099200 | tf_op jit(solution)/shard_map/gather | solution.py:48
  202.2 0.0 reduce-scatter.2.cloned.1.call-done
  202.2 1.4 add_convert_fusion
  203.6 0.8 fusion.16
  (3 shorter events, 0.0 us)
Async XLA Ops:
  7.2 4.3 %copy-start = (bf16[512,2048]{1,0:T(8,128)(2,1)S(1)}, bf16[512,2048]{1,0:T(8,128)(2,1)}, u32[]{:S(2)}) copy-start(bf16[512,2048]{1,0:T(8,128)(2,1)} %param.6) | copy-start | bytes 6291460
  17.5 100.6 %all-to-all-start = ((bf16[8,16,8,2048]{3,2,1,0:T(8,128)(2,1)}), bf16[8,16,8,2048]{3,2,1,0:T(8,128)(2,1)}, u32[]{:S(2)}, u32[]{:S(2)}) async-start(bf16[8,16,8,2048]{3,2,1,0:T(8,128)(2,1)} %bitcast.39), calls=%async_computation.1 | async-start | bytes 8388608 | tf_op jit(solution)/shard_map/all_to_all | solution.py:34
  24.8 177.4 %reduce-scatter.2.cloned.1.call-start = ((), (), s32[]{:S(2)}) async-start(), calls=%async_computation.3 | async-start | bytes 5242880 | tf_op jit(solution)/shard_map/reduce_scatter | solution.py:59
  145.2 53.4 %all-to-all-start.1 = ((f32[8,16,8,512]{3,2,1,0:T(8,128)}), f32[8,16,8,512]{3,2,1,0:T(8,128)}, u32[]{:S(2)}, u32[]{:S(2)}) async-start(f32[8,16,8,512]{3,2,1,0:T(8,128)} %copy.21), calls=%async_computation.2 | async-start | bytes 4194304 | tf_op jit(solution)/shard_map/all_to_all | solution.py:47
Sparse Core Ops, SparseCore 0:
  57.8 45.7 reduce-scatter.1
